TPU v7x, 128 devices: a whole 4x4x4 slice. The times are simulated.
128 devices in a mesh: gx: 8 (over z, core), gy: 16 (over x, y).
Axes of the slice: x: 4, y: 4, z: 4, core: 2. Of those that a mesh axis runs over, the one named last changes fastest.
Arguments:
- policy_logp: float32 [16, 2048, 4096], P('gy', 'gx'), may hold values from -2 to 0
- anchor_logp: float32 [16, 2048, 4096], P('gy', 'gx'), may hold values from -2 to 0
- lengths: int32 [16, 2048], P('gy', 'gx'), may hold values from 512 to 4096
- rewards: int32 [16, 2048], P('gy', 'gx'), may hold values from 0 to 8
- slot_prompt: int32 [16, 2048], P('gy', 'gx'), may hold values from 0 to 2047, as said below
Outputs:
- token_grad: float32 [16, 2048, 4096], P(None, ('gx', 'gy'))
- sample_loss: float32 [16, 2048], P(None, ('gx', 'gy'))
- advantage: float32 [16, 2048], P(None, ('gx', 'gy'))
Inputs may be any that keep to these rules, and one draw needn't show every extreme that they name: `slot_prompt`: for every member k and every aligned block of 256 slots, the slots of the block hold each prompt of the same block exactly once.
All inputs are finite; a program needn't handle non-finite values.
Results may differ from a plain program's by a relative error of at most 0.00002.
Values sent between devices are 32-bit elements; how exact they have to be, the bound alone decides.
A program may use at most 64 MiB of HBM per device.

v0:
```python
import jax
import jax.numpy as jnp
from jax import lax
from jax.sharding import Mesh
from jax.sharding import PartitionSpec as P

GX_GY = ("gx_0", "gx_1", "gy_0", "gy_1")
GY = ("gy_0", "gy_1")
GX = ("gx_0", "gx_1")
kl_weight = 0.1


def by_axis(x, axes):
    for axis in axes:
        x = lax.psum(x, axis)
    return x


def sent_together(arrays, axis, split_dim, concat_dim, along):
    columns = [a.reshape(*a.shape[:along], -1) for a in arrays]
    both = jnp.concatenate(columns, axis=along)
    out, at, gathered = (
        lax.all_to_all(both, axis, split_axis=split_dim, concat_axis=concat_dim, tiled=True),
        0,
        [],
    )
    for a, column in zip(arrays, columns):
        piece = out[..., at : at + column.shape[along]]
        gathered.append(piece.reshape(*piece.shape[:along], *a.shape[along:]))
        at += column.shape[along]
    return tuple(gathered)


def score_tokens(policy, anchor, seq_len, reward, total, members, grad_scale, loss_scale):
    advantage = (members * reward - total[None, :]) / (members - 1)
    positions = lax.broadcasted_iota(jnp.float32, policy.shape, 2)
    valid = positions < seq_len[:, :, None]
    log_ratio = anchor - policy
    ratio = jnp.exp(log_ratio)
    token_term = -advantage[:, :, None] * policy + kl_weight * (ratio - log_ratio - 1.0)
    token_grad = (
        jnp.where(valid, -advantage[:, :, None] + kl_weight * (1.0 - ratio), 0.0) * grad_scale
    )
    sample_loss = jnp.sum(jnp.where(valid, token_term, 0.0), axis=2) * loss_scale
    return (token_grad, sample_loss, advantage)


def body(policy_logp, anchor_logp, lengths, rewards, slot_prompt):
    members_dev, slots, seq_slots = policy_logp.shape
    local_prompt = slot_prompt % slots
    member_rows = lax.broadcasted_iota(jnp.int32, (members_dev, slots), 0)
    slot_ids = lax.broadcasted_iota(jnp.int32, (members_dev, slots), 1)
    inverse = jnp.zeros((members_dev, slots), jnp.int32).at[member_rows, local_prompt].set(slot_ids)
    sorted_policy = jnp.take_along_axis(policy_logp, inverse[:, :, None], axis=1)
    sorted_anchor = jnp.take_along_axis(anchor_logp, inverse[:, :, None], axis=1)
    sorted_len = jnp.take_along_axis(lengths, inverse, axis=1).astype(jnp.float32)
    sorted_reward = jnp.take_along_axis(rewards, inverse, axis=1).astype(jnp.float32) * 0.25
    count_local = jnp.sum(lengths.astype(jnp.float32))
    token_total = by_axis(count_local, GX_GY)
    members = members_dev * lax.axis_size(GY)
    samples = members * slots * lax.axis_size(GX)
    grad_scale = samples * seq_slots / token_total
    loss_scale = samples / token_total
    member_sums = jnp.sum(sorted_reward, axis=0)
    total = by_axis(member_sums, GY)
    token_grad, sample_loss, advantage = score_tokens(
        sorted_policy,
        sorted_anchor,
        sorted_len,
        sorted_reward,
        total,
        members,
        grad_scale,
        loss_scale,
    )
    return sent_together((token_grad, sample_loss, advantage), GY, 1, 0, 2)


def solution(mesh):
    torus = Mesh(mesh.devices.reshape(4, 2, 4, 4), ("gx_0", "gx_1", "gy_0", "gy_1"))
    return jax.shard_map(
        body,
        mesh=torus,
        in_specs=(P(GY, GX, None), P(GY, GX, None), P(GY, GX), P(GY, GX), P(GY, GX)),
        out_specs=(P(None, GX_GY, None), P(None, GX_GY), P(None, GX_GY)),
        check_vma=False,
    )
```

profile of v0, /device:TPU:0, one launch (start us, length us, event | category | flops | bytes accessed | tf_op | source)
XLA Modules:
  0.0 137.0 jit_solution(9556072892073195460)
XLA Ops:
  0.6 0.0 copy-start
  0.6 1.3 convert_reduce_fusion
  1.9 12.5 %psum.44 = f32[]{:T(128)} all-reduce(f32[]{:T(128)} %convert_reduce_fusion), channel_id=1, replica_groups=mesh['gx_0'=4,'gx_1'=2,'gy_0'=4,'gy_1'=4] {'gx_0'}, use_global_device_ids=true, to_apply=%region_4.7 | all-reduce | flops 1 | bytes 8 | tf_op jit(solution)/shard_map/psum | solution.py:15
  14.4 3.1 %psum.45 = f32[]{:T(128)} all-reduce(f32[]{:T(128)} %psum.44), channel_id=1, replica_groups=mesh['gx_0'=4,'gx_1'=2,'gy_0'=4,'gy_1'=4] {'gx_1'}, use_global_device_ids=true, to_apply=%region_5.8 | all-reduce | flops 1 | bytes 8 | tf_op jit(solution)/shard_map/psum | solution.py:15
  17.5 0.7 fusion.11
  18.2 1.4 %scatter_custom_fusion = s32[256]{0:T(256)S(1)} fusion(s32[256]{0:T(256)S(1)} %bitcast.61, s32[256]{0:T(256)S(1)} %iota.12, s32[]{:T(128)} %constant.18.clone.1), kind=kCustom, calls=%fused_computation.40 | custom fusion | bytes 1028 | tf_op jit(solution)/shard_map/scatter | solution.py:53
  19.7 0.0 copy-done
  19.7 1.9 %gather_fusion.1 = s32[256]{0:T(256)S(1)} fusion(s32[256]{0:T(256)S(1)} %bitcast.41, s32[1024]{0:T(1024)S(1)} %pad_clamp_fusion.1), kind=kCustom, calls=%fused_computation.2.clone | custom fusion | bytes 3072 | tf_op jit(solution)/shard_map/jit(take_along_axis)/gather | solution.py:57
  21.7 2.0 %gather_fusion = s32[256]{0:T(256)S(1)} fusion(s32[256]{0:T(256)} %bitcast.42, s32[1024]{0:T(1024)S(1)} %pad_clamp_fusion.1), kind=kCustom, calls=%fused_computation.clone | custom fusion | bytes 3072 | tf_op jit(solution)/shard_map/jit(take_along_axis)/gather | solution.py:56
  23.7 11.1 %all-reduce.2 = (f32[]{:T(128)}, f32[256]{0:T(256)S(1)}) all-reduce(f32[]{:T(128)} %psum.45, f32[256]{0:T(256)S(1)} %bitcast.62), channel_id=1, replica_groups=mesh['gx_0'=4,'gx_1'=2,'gy_0'=4,'gy_1'=4] {'gy_0'}, use_global_device_ids=true, to_apply=%region_6.9 | all-reduce | flops 257 | bytes 2056 | tf_op jit(solution)/shard_map/psum | solution.py:15
  34.8 11.3 %all-reduce.1 = (f32[]{:T(128)}, f32[1,256]{1,0:T(1,128)S(1)}) all-reduce(f32[]{:T(128)} %get-tuple-element.9, f32[1,256]{1,0:T(1,128)S(1)} %bitcast.63), channel_id=1, replica_groups=mesh['gx_0'=4,'gx_1'=2,'gy_0'=4,'gy_1'=4] {'gy_1'}, use_global_device_ids=true, to_apply=%region_7.10 | all-reduce | flops 257 | bytes 2056 | tf_op jit(solution)/shard_map/psum | solution.py:15
  47.5 0.1 copy.23
  47.7 7.9 %gather_fusion.3 = f32[256,4096]{1,0:T(8,128)} fusion(f32[256,4096]{1,0:T(8,128)} %bitcast.43, s32[1024]{0:T(1024)S(1)} %pad_clamp_fusion), kind=kCustom, calls=%fused_computation.3.clone | custom fusion | bytes 8389632 | tf_op jit(solution)/shard_map/jit(take_along_axis)/gather | solution.py:54
  55.6 7.8 %gather_fusion.2 = f32[256,4096]{1,0:T(8,128)} fusion(f32[256,4096]{1,0:T(8,128)} %bitcast.44, s32[1024]{0:T(1024)S(1)} %pad_clamp_fusion), kind=kCustom, calls=%fused_computation.1.clone | custom fusion | bytes 8389632 | tf_op jit(solution)/shard_map/jit(take_along_axis)/gather | solution.py:55
  63.4 6.4 %fusion.8 = (f32[256]{0:T(256)S(1)}, f32[1,256,4096]{2,1,0:T(8,128)}) fusion(f32[256,4096]{1,0:T(8,128)} %gather_fusion.3, f32[256,4096]{1,0:T(8,128)} %gather_fusion.2, f32[256]{0:T(256)S(1)} %bitcast.55, f32[256]{0:T(256)S(1)} %bitcast.54, pred[256]{0:T(512)(128)(4,1)S(1)} %get-tuple-element.11, f32[]{:T(128)S(6)} %div.14), kind=kLoop, calls=%fused_computation.15 | loop fusion | flops 16776960 | bytes 12586244 | tf_op jit(solution)/shard_map/reduce_sum | solution.py:44
  69.7 0.1 copy.22
  69.9 5.6 %concatenate.7 = f32[1,256,4098]{2,1,0:T(8,128)} concatenate(f32[1,256,4096]{2,1,0:T(8,128)} %get-tuple-element.16, f32[1,256,1]{2,1,0:T(8,128)S(1)} %copy.22, f32[1,256,1]{2,1,0:T(8,128)S(1)} %copy.23), dimensions={2} | concatenate | bytes 8392704 | tf_op jit(solution)/shard_map/concatenate | solution.py:21
  75.5 6.7 %copy.24 = f32[1,256,4098]{2,0,1:T(1,128)S(1)} copy(f32[1,256,4098]{2,1,0:T(8,128)} %concatenate.7) | data formatting | bytes 8392704 | tf_op jit(solution)/shard_map/concatenate | solution.py:21
  82.1 51.2 %all_to_all.12 = f32[1,256,4098]{2,0,1:T(1,128)S(1)} all-to-all(f32[1,256,4098]{2,0,1:T(1,128)S(1)} %copy.24), channel_id=1, replica_groups=mesh['gx_0'=4,'gx_1'=2,'gy_0'=4,'gy_1'=4] {'gy_0','gy_1'}, dimensions={1} | all-to-all | bytes 8392704 | tf_op jit(solution)/shard_map/all_to_all | solution.py:23
  133.4 0.3 copy.25
  133.7 0.8 slice_reduce_fusion
  134.5 2.5 %slice.24 = f32[16,16,4096]{2,1,0:T(8,128)} slice(f32[16,16,4098]{2,1,0:T(8,128)S(1)} %bitcast.46), slice={[0:16], [0:16], [0:4096]} | slice | bytes 8388608 | tf_op jit(solution)/shard_map/slice | solution.py:28
  (11 shorter events, 0.1 us)
Async XLA Ops:
  0.6 19.1 %copy-start = (s32[1,256]{1,0:T(1,128)S(1)}, s32[1,256]{1,0:T(1,128)}, u32[]{:S(2)}) copy-start(s32[1,256]{1,0:T(1,128)} %param.12) | copy-start | bytes 3076
where the time goes:
time: 138 us; the launch traced here: 137 us
  blocking collectives  89.3 us (65%)
  local copies, waits for them, and re-layouts  37.2 us (27%)
  other arithmetic  8.42 us (6%)
  between operations  2.11 us (2%)
    all_to_all x1, blocking collectives, sent_together(): lax.all_to_all(both, axis, split_axis=split_dim, concat_axis=concat_dim,...  51.2 us
    psum x4, blocking collectives, by_axis(): x = lax.psum(x, axis)  38 us
    concatenate x2, local copies, waits for them, and re-layouts, sent_together(): both = jnp.concatenate(columns, axis=along)  12.2 us
    gather x1, local copies, waits for them, and re-layouts, body(): jnp.take_along_axis(policy_logp, inverse[:, :, None], axis=1)  7.89 us
    gather x1, local copies, waits for them, and re-layouts, body(): jnp.take_along_axis(anchor_logp, inverse[:, :, None], axis=1)  7.8 us
    reduce_sum x1, other arithmetic, score_tokens(): jnp.sum(jnp.where(valid, token_term, 0.0), axis=2) * loss_scale  6.36 us
    slice x2, local copies, waits for them, and re-layouts, sent_together(): piece = out[..., at:at + column.shape[along]]  3.33 us

commit v1 on v0

--- a/solution.py
+++ b/solution.py
@@ -12,7 +12,7 @@
 
 def by_axis(x, axes):
     for axis in axes:
-        x = lax.psum(x, axis)
+        x = jnp.sum(lax.all_gather(x, axis), axis=0)
     return x
 
 

time: 138 us -> 160 us (1.16)
  local copies, waits for them, and re-layouts: 37.2 us -> 47.7 us
  blocking collectives: 89.3 us -> 98.4 us
  other arithmetic: 8.42 us -> 10.9 us
    psum x4 -> x0, blocking collectives: 38 us -> none  [by_axis(): x = lax.psum(x, axis)]
    unnamed x0 -> x4, blocking collectives: none -> 35.5 us
    all_gather x0 -> x2, blocking collectives: none -> 14 us  [by_axis(): x = jnp.sum(lax.all_gather(x, axis), axis=0)]
    unnamed x3 -> x15, local copies, waits for them, and re-layouts: 0.29 us -> 10.8 us
    reduce_sum x0 -> x6, other arithmetic: none -> 2.46 us  [by_axis(): x = jnp.sum(lax.all_gather(x, axis), axis=0)]
    all_to_all x1, blocking collectives: 51.2 us -> 49 us  [sent_together(): lax.all_to_all(both, axis, split_axis=split_dim, concat_axis=concat_dim,...]
where the time goes in v1:
time: 160 us; the launch traced here: 159 us
  blocking collectives  98.4 us (62%)
  local copies, waits for them, and re-layouts  47.7 us (30%)
  other arithmetic  10.9 us (7%)
  between operations  2.13 us (1%)
    all_to_all x1, blocking collectives, sent_together(): lax.all_to_all(both, axis, split_axis=split_dim, concat_axis=concat_dim,...  49 us
    unnamed x4, blocking collectives  35.5 us
    all_gather x2, blocking collectives, by_axis(): x = jnp.sum(lax.all_gather(x, axis), axis=0)  14 us
    concatenate x2, local copies, waits for them, and re-layouts, sent_together(): both = jnp.concatenate(columns, axis=along)  12.2 us
    unnamed x15, local copies, waits for them, and re-layouts  10.8 us
    gather x1, local copies, waits for them, and re-layouts, body(): jnp.take_along_axis(policy_logp, inverse[:, :, None], axis=1)  7.89 us
    gather x1, local copies, waits for them, and re-layouts, body(): jnp.take_along_axis(anchor_logp, inverse[:, :, None], axis=1)  7.8 us
    reduce_sum x1, other arithmetic, score_tokens(): jnp.sum(jnp.where(valid, token_term, 0.0), axis=2) * loss_scale  6.36 us

profile of v1, /device:TPU:0, one launch (start us, length us, event | category | flops | bytes accessed | tf_op | source)
XLA Modules:
  0.0 159.2 jit_solution(11853387283083455092)
XLA Ops:
  0.7 1.3 convert_reduce_fusion
  3.2 1.4 dynamic-update-slice
  4.6 1.2 dynamic-slice.1
  5.8 11.8 %all-reduce.1 = f32[4]{0:T(128)S(1)} all-reduce(f32[4]{0:T(128)S(1)} %dynamic-update-slice), channel_id=1, replica_groups=mesh['gx_0'=4,'gx_1'=2,'gy_0'=4,'gy_1'=4] {'gx_0'}, use_global_device_ids=true, to_apply=%add.1 | all-reduce | flops 4 | bytes 32
  18.3 1.4 dynamic-update-slice.1
  19.7 1.2 dynamic-slice.2
  20.9 2.4 %all-reduce.2 = f32[2]{0:T(128)S(1)} all-reduce(f32[2]{0:T(128)S(1)} %dynamic-update-slice.1), channel_id=1, replica_groups=mesh['gx_0'=4,'gx_1'=2,'gy_0'=4,'gy_1'=4] {'gx_1'}, use_global_device_ids=true, to_apply=%add.2 | all-reduce | flops 2 | bytes 16
  24.0 1.4 dynamic-update-slice.2
  25.4 1.2 dynamic-slice.3
  26.6 10.5 %all-reduce.3 = f32[4]{0:T(128)S(1)} all-reduce(f32[4]{0:T(128)S(1)} %dynamic-update-slice.2), channel_id=1, replica_groups=mesh['gx_0'=4,'gx_1'=2,'gy_0'=4,'gy_1'=4] {'gy_0'}, use_global_device_ids=true, to_apply=%add.3 | all-reduce | flops 4 | bytes 32
  37.7 1.4 dynamic-update-slice.3
  39.1 10.7 %all-reduce.4 = f32[4]{0:T(128)S(1)} all-reduce(f32[4]{0:T(128)S(1)} %dynamic-update-slice.3), channel_id=1, replica_groups=mesh['gx_0'=4,'gx_1'=2,'gy_0'=4,'gy_1'=4] {'gy_1'}, use_global_device_ids=true, to_apply=%add.4 | all-reduce | flops 4 | bytes 32
  52.5 1.4 scatter_custom_fusion
  54.0 1.9 %gather_fusion.1 = s32[256]{0:T(256)S(1)} fusion(s32[256]{0:T(256)S(1)} %bitcast.51, s32[1024]{0:T(1024)S(1)} %pad_clamp_fusion.1), kind=kCustom, calls=%fused_computation.2.clone | custom fusion | bytes 3072 | tf_op jit(solution)/shard_map/jit(take_along_axis)/gather | solution.py:57
  55.9 2.0 %gather_fusion = s32[256]{0:T(256)S(1)} fusion(s32[256]{0:T(256)} %bitcast.52, s32[1024]{0:T(1024)S(1)} %pad_clamp_fusion.1), kind=kCustom, calls=%fused_computation.clone | custom fusion | bytes 3072 | tf_op jit(solution)/shard_map/jit(take_along_axis)/gather | solution.py:56
  57.9 7.0 %all-gather.1 = f32[4,1,256]{2,1,0:T(1,128)S(1)} all-gather(f32[1,1,256]{2,1,0:T(1,128)S(1)} %multiply_bitcast_fusion), channel_id=1, replica_groups=mesh['gx_0'=4,'gx_1'=2,'gy_0'=4,'gy_1'=4] {'gy_0'}, dimensions={0}, use_global_device_ids=true | all-gather | bytes 5120 | tf_op jit(solution)/shard_map/all_gather | solution.py:15
  65.0 7.0 %all-gather.2 = f32[4,1,256]{2,1,0:T(1,128)S(1)} all-gather(f32[1,1,256]{2,1,0:T(1,128)S(1)} %bitcast.71), channel_id=2, replica_groups=mesh['gx_0'=4,'gx_1'=2,'gy_0'=4,'gy_1'=4] {'gy_1'}, dimensions={0}, use_global_device_ids=true | all-gather | bytes 5120 | tf_op jit(solution)/shard_map/all_gather | solution.py:15
  72.1 7.9 %gather_fusion.3 = f32[256,4096]{1,0:T(8,128)} fusion(f32[256,4096]{1,0:T(8,128)} %bitcast.53, s32[1024]{0:T(1024)S(1)} %pad_clamp_fusion), kind=kCustom, calls=%fused_computation.3.clone | custom fusion | bytes 8389632 | tf_op jit(solution)/shard_map/jit(take_along_axis)/gather | solution.py:54
  80.0 7.8 %gather_fusion.2 = f32[256,4096]{1,0:T(8,128)} fusion(f32[256,4096]{1,0:T(8,128)} %bitcast.54, s32[1024]{0:T(1024)S(1)} %pad_clamp_fusion), kind=kCustom, calls=%fused_computation.1.clone | custom fusion | bytes 8389632 | tf_op jit(solution)/shard_map/jit(take_along_axis)/gather | solution.py:55
  87.8 6.4 %fusion.8 = (f32[256]{0:T(256)S(1)}, f32[1,256,4096]{2,1,0:T(8,128)}) fusion(f32[256,4096]{1,0:T(8,128)} %gather_fusion.3, f32[256,4096]{1,0:T(8,128)} %gather_fusion.2, f32[256]{0:T(256)S(1)} %bitcast.65, f32[256]{0:T(256)S(1)} %bitcast.64, pred[256]{0:T(512)(128)(4,1)S(1)} %get-tuple-element.7, f32[]{:T(128)S(6)} %div.14), kind=kLoop, calls=%fused_computation.15 | loop fusion | flops 16776960 | bytes 12586244 | tf_op jit(solution)/shard_map/reduce_sum | solution.py:44
  94.3 5.6 %concatenate.7 = f32[1,256,4098]{2,1,0:T(8,128)} concatenate(f32[1,256,4096]{2,1,0:T(8,128)} %get-tuple-element.12, f32[1,256,1]{2,1,0:T(8,128)S(1)} %copy.22, f32[1,256,1]{2,1,0:T(8,128)S(1)} %copy.23), dimensions={2} | concatenate | bytes 8392704 | tf_op jit(solution)/shard_map/concatenate | solution.py:21
  99.9 6.7 %copy.24 = f32[1,256,4098]{2,0,1:T(1,128)S(1)} copy(f32[1,256,4098]{2,1,0:T(8,128)} %concatenate.7) | data formatting | bytes 8392704 | tf_op jit(solution)/shard_map/concatenate | solution.py:21
  106.6 49.0 %all_to_all.12 = f32[1,256,4098]{2,0,1:T(1,128)S(1)} all-to-all(f32[1,256,4098]{2,0,1:T(1,128)S(1)} %copy.24), channel_id=1, replica_groups=mesh['gx_0'=4,'gx_1'=2,'gy_0'=4,'gy_1'=4] {'gy_0','gy_1'}, dimensions={1} | all-to-all | bytes 8392704 | tf_op jit(solution)/shard_map/all_to_all | solution.py:23
  156.7 2.5 %slice.24 = f32[16,16,4096]{2,1,0:T(8,128)} slice(f32[16,16,4098]{2,1,0:T(8,128)S(1)} %bitcast.56), slice={[0:16], [0:16], [0:4096]} | slice | bytes 8388608 | tf_op jit(solution)/shard_map/slice | solution.py:28
  (29 shorter events, 5.9 us)
Async XLA Ops:
  0.6 53.3 %copy-start = (s32[1,256]{1,0:T(1,128)S(1)}, s32[1,256]{1,0:T(1,128)}, u32[]{:S(2)}) copy-start(s32[1,256]{1,0:T(1,128)} %param.12) | copy-start | bytes 3076
